TPU v7x, 512 devices: a whole 4x4x16 slice. The times are simulated.
512 devices in a mesh: prow: 16 (over z), pcol: 32 (over x, y, core).
Axes of the slice: x: 4, y: 4, z: 16, core: 2. Of those that a mesh axis runs over, the one named last changes fastest.
Arguments:
- matrix: float32 [8192, 32768], P('prow', 'pcol'), may hold values from -6 to 6
- pivot_inverse: float32 [2, 512, 512], P(None, 'prow'), may hold values from -0.01171875 to 0.01171875
- row_live: int32 [2, 16], replicated, may hold values 0 or 1
- col_live: int32 [2, 64], replicated, may hold values 0 or 1
Outputs:
- factored: float32 [8192, 32768], P('prow', 'pcol')
All inputs are finite; a program needn't handle non-finite values.
Results may differ from a plain program's by a relative error of at most 0.0001.
Values sent between devices are 32-bit elements; how exact they have to be, the bound alone decides.
No kernel may reach another device: no remote copies, remote signals or barrier semaphores. Data moves between devices by JAX's collectives and lax.ppermute only.
A program may use at most 64 MiB of HBM per device.

v0:
```python
import jax
import jax.numpy as jnp
from jax import lax
from jax.sharding import PartitionSpec as P


def copy_for_each(value, axis):
    copies = jnp.broadcast_to(value, (lax.axis_size(axis), *value.shape))
    return lax.all_to_all(copies, axis, split_axis=0, concat_axis=0, tiled=True)


def laid_out(tiles, dim):
    tiles = jnp.moveaxis(tiles, 0, dim)
    dims = tiles.shape
    return tiles.reshape(*dims[:dim], dims[dim] * dims[dim + 1], *dims[dim + 2 :])


def gathered_copies(value, axis, dim):
    tiles = copy_for_each(value, axis)
    return laid_out(tiles, dim)


def spread(value, axis, source):
    kept = jnp.where(lax.axis_index(axis) == source, value, 0).astype(value.dtype)
    return lax.psum(kept, axis)


def filled_up(lines, length):
    spare = -lines.shape[0] % length
    if not spare:
        return lines
    return jnp.concatenate([lines, jnp.zeros((spare, *lines.shape[1:]), lines.dtype)])


def broadcast_by_parts(value, axis, root):
    lines = jnp.where(lax.axis_index(axis) == root, value, jnp.zeros_like(value)).reshape(
        -1, *value.shape[1:][-1:]
    )
    padded = filled_up(lines, lax.axis_size(axis))
    own = lax.psum_scatter(padded, axis, scatter_dimension=0, tiled=True)
    return lax.all_gather(own, axis, axis=0, tiled=True)[: len(lines)].reshape(value.shape)


def apply_pivot(column_part, pivot_rows):
    return jnp.einsum(
        "rbc,cd->rbd",
        column_part,
        gathered_copies(pivot_rows, "prow", 0),
        precision=lax.Precision.HIGHEST,
    )


def per_device(matrix, pivot_inverse, row_live, col_live):
    block_width = pivot_inverse.shape[2]
    row_blocks = matrix.shape[0] // block_width
    col_blocks = matrix.shape[1] // block_width
    pcol_here = lax.axis_index("pcol")
    row_index = jnp.arange(row_blocks, dtype=jnp.int32) * lax.axis_size("prow") + lax.axis_index(
        "prow"
    )
    col_index = jnp.arange(col_blocks, dtype=jnp.int32) * lax.axis_size("pcol") + pcol_here
    blocks = matrix.reshape(row_blocks, block_width, col_blocks, block_width)

    def lower_panel(column_part, panel):
        row_mask = jnp.where(row_index > panel, jnp.take(row_live[panel], row_index), 0).astype(
            jnp.float32
        )[:, None, None]
        received = spread(column_part, "pcol", panel)
        return apply_pivot(received, pivot_inverse[panel]) * row_mask

    def upper_row(current, panel):
        col_mask = jnp.where(col_index > panel, jnp.take(col_live[panel], col_index), 0).astype(
            jnp.float32
        )
        return broadcast_by_parts(current[0] * col_mask[None, :, None], "prow", panel)

    def store_lower(column_part, lower_part, panel):
        keep_rows = (row_index > panel)[:, None, None] & (pcol_here == panel)
        return jnp.where(keep_rows, lower_part, column_part)

    def outer_update(current, lower_part, upper_part):
        return current - jnp.einsum(
            "rbc,cjd->rbjd", lower_part, upper_part, precision=lax.Precision.HIGHEST
        )

    lower_part = lower_panel(blocks[:, :, 0, :], 0)
    upper_part = upper_row(blocks, 0)
    blocks = outer_update(blocks, lower_part, upper_part)
    blocks = blocks.at[:, :, 0, :].set(store_lower(blocks[:, :, 0, :], lower_part, 0))
    next_lower = lower_panel(blocks[:, :, 0, :], 1)
    next_upper = upper_row(blocks, 1)
    blocks = outer_update(blocks, next_lower, next_upper)
    blocks = blocks.at[:, :, 0, :].set(store_lower(blocks[:, :, 0, :], next_lower, 1))
    return blocks.reshape(row_blocks * block_width, col_blocks * block_width)


def solution(mesh):
    in_specs = (P("prow", "pcol"), P(None, "prow", None), P(), P())
    out_specs = P("prow", "pcol")
    return jax.shard_map(
        per_device, mesh=mesh, in_specs=in_specs, out_specs=out_specs, check_vma=False
    )
```

profile of v0, /device:TPU:4, one launch (start us, length us, event | category | flops | bytes accessed | tf_op | source)
XLA Modules:
  0.0 403.3 jit_solution(14999764444500926546)
XLA Ops:
  9.6 1.7 squeeze_reshape.3
  11.4 1.5 multiply_select_fusion.1
  13.0 1.5 copy-done
  14.5 2.8 reshape.162
  17.3 2.5 broadcast_select_fusion
  19.8 1.1 copy.28
  20.9 1.1 broadcast_in_dim.55
  22.0 15.2 %all-to-all-start = ((f32[16,32,512]{2,1,0:T(8,128)}), f32[16,32,512]{2,1,0:T(8,128)S(1)}, u32[]{:S(2)}, u32[]{:S(2)}) async-start(f32[16,32,512]{2,1,0:T(8,128)} %broadcast_in_dim.55), calls=%async_computation | async-start | bytes 2097152 | tf_op jit(solution)/shard_map/all_to_all | solution.py:9
  37.2 85.9 %reduce-scatter.3.cloned.1.call-done = f32[64,512]{1,0:T(8,128)} async-done(((f32[1024,512]{1,0:T(8,128)}), f32[64,512]{1,0:T(8,128)}) %reduce-scatter.3.cloned.1.call-update) | async-done | bytes 131088 | tf_op jit(solution)/shard_map/reduce_scatter | solution.py:40
  123.4 1.8 copy.7
  126.5 2.9 copy.9
  129.6 32.3 %all-reduce.3.cloned.1.call-done = f32[512,512]{1,0:T(8,128)} async-done(((f32[512,512]{1,0:T(8,128)}), f32[512,512]{1,0:T(8,128)}) %all-reduce.3.cloned.1.call-update) | async-done | bytes 1048592 | tf_op jit(solution)/shard_map/psum | solution.py:25
  162.0 1.0 copy-done.1
  162.9 3.4 convolution_multiply_fusion.1
  166.3 29.4 %all-gather.3.cloned.1.call-done = f32[1024,512]{1,0:T(8,128)} async-done(((f32[64,512]{1,0:T(8,128)}), f32[1024,512]{1,0:T(8,128)}) %all-gather.3.cloned.1.call-update) | async-done | bytes 2097168 | tf_op jit(solution)/shard_map/all_gather | solution.py:41
  195.8 3.4 reshape.165
  199.2 5.9 %subtract_bitcast_fusion = f32[1,512,2,512]{3,1,2,0:T(8,128)S(1)} fusion(f32[512,2,512]{2,0,1:T(8,128)} %copy.9, f32[512,2,512]{2,1,0:T(2,128)} %reshape.165, f32[512,512]{1,0:T(8,128)S(1)} %convolution_multiply_fusion.1), kind=kOutput, calls=%fused_computation.8 | convolution fusion | flops 3221749760 | bytes 7340032 | tf_op jit(solution)/shard_map/rbc,cjd->rbjd/dot_general | solution.py:82
  205.1 1.2 broadcast_select_fusion.1
  206.4 2.9 copy.11
  209.3 3.7 squeeze.35
  213.0 3.1 multiply_select_fusion
  216.7 1.1 broadcast_in_dim.61
  217.8 8.2 %all-to-all-start.1 = ((f32[16,32,512]{2,1,0:T(8,128)}), f32[16,32,512]{2,1,0:T(8,128)S(1)}, u32[]{:S(2)}, u32[]{:S(2)}) async-start(f32[16,32,512]{2,1,0:T(8,128)} %broadcast_in_dim.61), calls=%async_computation.2 | async-start | bytes 2097152 | tf_op jit(solution)/shard_map/all_to_all | solution.py:9
  226.2 80.7 %reduce-scatter.5.cloned.1.call-done = f32[64,512]{1,0:T(8,128)} async-done(((f32[1024,512]{1,0:T(8,128)}), f32[64,512]{1,0:T(8,128)}) %reduce-scatter.5.cloned.1.call-update) | async-done | bytes 131088 | tf_op jit(solution)/shard_map/reduce_scatter | solution.py:40
  307.6 45.7 %all-reduce.5.cloned.1.call-done = f32[512,512]{1,0:T(8,128)} async-done(((f32[512,512]{1,0:T(8,128)}), f32[512,512]{1,0:T(8,128)}) %all-reduce.5.cloned.1.call-update) | async-done | bytes 1048592 | tf_op jit(solution)/shard_map/psum | solution.py:25
  353.3 3.4 convolution_multiply_fusion
  356.7 23.4 %all-gather.5.cloned.1.call-done = f32[1024,512]{1,0:T(8,128)} async-done(((f32[64,512]{1,0:T(8,128)}), f32[1024,512]{1,0:T(8,128)}) %all-gather.5.cloned.1.call-update) | async-done | bytes 2097168 | tf_op jit(solution)/shard_map/all_gather | solution.py:41
  380.0 3.4 reshape.168
  383.5 6.6 %bitcast_subtract_fusion = f32[1,512,2,512]{3,1,2,0:T(8,128)} fusion(f32[1,512,2,512]{3,1,2,0:T(8,128)S(1)} %bitcast_dynamic-update-slice_fusion, f32[512,2,512]{2,1,0:T(2,128)} %reshape.168, f32[512,512]{1,0:T(8,128)S(1)} %convolution_multiply_fusion), kind=kOutput, calls=%fused_computation.2 | convolution fusion | flops 3221749760 | bytes 7340032 | tf_op jit(solution)/shard_map/rbc,cjd->rbjd/dot_general | solution.py:82
  390.1 2.4 fusion.10
  392.5 1.9 copy.14
  394.4 1.8 copy.15
  (36 shorter events, 4.4 us)
Async XLA Ops:
  7.4 115.8 %reduce-scatter.3.cloned.1.call-start = ((), (), s32[]{:S(2)}) async-start(), calls=%async_computation.5 | async-start | bytes 2228224 | tf_op jit(solution)/shard_map/reduce_scatter | solution.py:40
  12.9 1.6 copy-start
  12.9 149.0 %all-reduce.3.cloned.1.call-start = ((), (), s32[]{:S(2)}) async-start(), calls=%async_computation.4 | async-start | bytes 2097152 | tf_op jit(solution)/shard_map/psum | solution.py:25
  19.8 1.1 copy-start.3
  22.0 140.0 %all-to-all-start = ((f32[16,32,512]{2,1,0:T(8,128)}), f32[16,32,512]{2,1,0:T(8,128)S(1)}, u32[]{:S(2)}, u32[]{:S(2)}) async-start(f32[16,32,512]{2,1,0:T(8,128)} %broadcast_in_dim.55), calls=%async_computation | async-start | bytes 2097152 | tf_op jit(solution)/shard_map/all_to_all | solution.py:9
  37.2 158.6 %all-gather.3.cloned.1.call-start = ((), (), s32[]{:S(2)}) async-start(), calls=%async_computation.6 | async-start | bytes 2228224 | tf_op jit(solution)/shard_map/all_gather | solution.py:41
  123.2 183.7 %reduce-scatter.5.cloned.1.call-start = ((), (), s32[]{:S(2)}) async-start(), calls=%async_computation.8 | async-start | bytes 2228224 | tf_op jit(solution)/shard_map/reduce_scatter | solution.py:40
  123.4 1.8 copy-start.4
  162.0 1.0 copy-start.1
  216.1 137.2 %all-reduce.5.cloned.1.call-start = ((), (), s32[]{:S(2)}) async-start(), calls=%async_computation.7 | async-start | bytes 2097152 | tf_op jit(solution)/shard_map/psum | solution.py:25
  217.8 89.8 %all-to-all-start.1 = ((f32[16,32,512]{2,1,0:T(8,128)}), f32[16,32,512]{2,1,0:T(8,128)S(1)}, u32[]{:S(2)}, u32[]{:S(2)}) async-start(f32[16,32,512]{2,1,0:T(8,128)} %broadcast_in_dim.61), calls=%async_computation.2 | async-start | bytes 2097152 | tf_op jit(solution)/shard_map/all_to_all | solution.py:9
  226.0 154.1 %all-gather.5.cloned.1.call-start = ((), (), s32[]{:S(2)}) async-start(), calls=%async_computation.9 | async-start | bytes 2228224 | tf_op jit(solution)/shard_map/all_gather | solution.py:41
  307.6 45.7 %copy-start.2 = (f32[16,32,512]{2,1,0:T(8,128)}, f32[16,32,512]{2,1,0:T(8,128)S(1)}, u32[]{:S(2)}) copy-start(f32[16,32,512]{2,1,0:T(8,128)S(1)} %all-to-all-done.1) | copy-start | bytes 3145732
Sparse Core Ops, SparseCore 0:
  13.1 110.0 reduce-scatter.2
  125.3 70.4 all-gather.2
  216.2 90.6 reduce-scatter.4
  308.8 71.1 all-gather.4
Sparse Core Ops, SparseCore 1:
  20.9 141.0 all-reduce.2
  219.8 133.4 all-reduce.4
where the time goes:
time: 404 us; the launch traced here: 403 us
  waiting for transfers between devices  298 us (74%)
  local copies, waits for them, and re-layouts  34.7 us (9%)
  starting transfers between devices  24 us (6%)
  matrix products  19.2 us (5%)
  between operations  16 us (4%)
  other arithmetic  11.4 us (3%)
    reduce_scatter x2, waiting for transfers between devices, broadcast_by_parts(): own = lax.psum_scatter(padded, axis, scatter_dimension=0, tiled=True)  167 us
    psum x2, waiting for transfers between devices, spread(): return lax.psum(kept, axis)  78 us
    all_gather x2, waiting for transfers between devices, broadcast_by_parts(): lax.all_gather(own, axis, axis=0, tiled=True)[:len(lines)]  52.8 us
    all_to_all x2, starting transfers between devices, copy_for_each(): return lax.all_to_all(copies, axis, split_axis=0, concat_axis=0, tiled=True)  23.4 us
    dot_general x2, matrix products, outer_update(): jnp.einsum('rbc,cjd->rbjd', lower_part, upper_part, precision=lax.Precisi...  12.4 us
  transfers between devices with their start and end apart: 8, of which 6 were waited for; matrix products, arithmetic and copies ran while one was open for 5% of the time, Pallas kernels for 0%

commit v1 on v0

--- a/solution.py
+++ b/solution.py
@@ -22,7 +22,7 @@
 
 def spread(value, axis, source):
     kept = jnp.where(lax.axis_index(axis) == source, value, 0).astype(value.dtype)
-    return lax.psum(kept, axis)
+    return jnp.sum(lax.all_gather(kept, axis), axis=0)
 
 
 def filled_up(lines, length):

time: 404 us -> 671 us (1.66)
  the two profiles are of different devices: /device:TPU:4 before, /device:TPU:1 now
where the time goes in v1:
time: 671 us; the launch traced here: 670 us
  waiting for transfers between devices  560 us (83%)
  other arithmetic  33.6 us (5%)
  local copies, waits for them, and re-layouts  28.8 us (4%)
  starting transfers between devices  17.3 us (3%)
  matrix products  15.3 us (2%)
  between operations  15.1 us (2%)
    all_gather x2, waiting for transfers between devices, spread(): return jnp.sum(lax.all_gather(kept, axis), axis=0)  261 us
    all_gather x2, waiting for transfers between devices, broadcast_by_parts(): lax.all_gather(own, axis, axis=0, tiled=True)[:len(lines)]  166 us
    reduce_scatter x2, waiting for transfers between devices, broadcast_by_parts(): own = lax.psum_scatter(padded, axis, scatter_dimension=0, tiled=True)  133 us
    reduce_sum x2, other arithmetic, spread(): return jnp.sum(lax.all_gather(kept, axis), axis=0)  24.5 us
    all_to_all x2, starting transfers between devices, copy_for_each(): return lax.all_to_all(copies, axis, split_axis=0, concat_axis=0, tiled=True)  17.1 us
  transfers between devices with their start and end apart: 8, of which 6 were waited for; matrix products, arithmetic and copies ran while one was open for 6% of the time, Pallas kernels for 0%

profile of v1, /device:TPU:1, one launch (start us, length us, event | category | flops | bytes accessed | tf_op | source)
XLA Modules:
  0.0 670.2 jit_solution(12565494323508194565)
XLA Ops:
  6.5 0.8 slice_bitcast_fusion.4
  8.8 1.7 squeeze_reshape.3
  10.5 1.5 multiply_select_fusion.1
  12.1 69.5 %reduce-scatter.3.cloned.1.call-done = f32[64,512]{1,0:T(8,128)} async-done(((f32[1024,512]{1,0:T(8,128)}), f32[64,512]{1,0:T(8,128)}) %reduce-scatter.3.cloned.1.call-update) | async-done | bytes 131088 | tf_op jit(solution)/shard_map/reduce_scatter | solution.py:40
  81.7 1.9 copy.25
  83.7 1.3 copy.27
  85.1 1.1 broadcast_in_dim.55
  86.2 8.5 %all-to-all-start = ((f32[16,32,512]{2,1,0:T(8,128)}), f32[16,32,512]{2,1,0:T(8,128)S(1)}, u32[]{:S(2)}, u32[]{:S(2)}) async-start(f32[16,32,512]{2,1,0:T(8,128)} %broadcast_in_dim.55), calls=%async_computation | async-start | bytes 2097152 | tf_op jit(solution)/shard_map/all_to_all | solution.py:9
  94.8 0.7 fusion.18
  96.4 1.8 copy.29
  98.2 81.8 %all-gather.7.cloned.1.call-done = f32[1024,512]{1,0:T(8,128)} async-done(((f32[64,512]{1,0:T(8,128)}), f32[1024,512]{1,0:T(8,128)}) %all-gather.7.cloned.1.call-update) | async-done | bytes 2097168 | tf_op jit(solution)/shard_map/all_gather | solution.py:41
  180.0 3.5 reshape.166
  183.5 130.1 %all-gather.11.cloned.1.call-done = f32[32,512,1,512]{3,1,2,0:T(8,128)} async-done(((f32[1,512,1,512]{3,1,2,0:T(8,128)}), f32[32,512,1,512]{3,1,2,0:T(8,128)}) %all-gather.11.cloned.1.call-update) | async-done | bytes 33554448 | tf_op jit(solution)/shard_map/all_gather | solution.py:25
  313.6 12.3 %reduce.6 = f32[512,512]{1,0:T(8,128)S(1)} reduce(f32[32,512,1,512]{3,1,2,0:T(8,128)} %all-gather.11.cloned.1.call-done, f32[]{:T(128)} %constant.92.clone.1), dimensions={0,2}, to_apply=%region_0.1 | reduce | flops 8126464 | bytes 34603012 | tf_op jit(solution)/shard_map/reduce_sum | solution.py:25
  325.9 1.9 convolution_multiply_fusion.1
  327.8 5.3 subtract_bitcast_fusion
  333.1 1.2 broadcast_select_fusion
  334.4 2.9 copy.31
  337.3 3.7 squeeze.35
  340.9 3.1 multiply_select_fusion
  344.1 63.1 %reduce-scatter.5.cloned.1.call-done = f32[64,512]{1,0:T(8,128)} async-done(((f32[1024,512]{1,0:T(8,128)}), f32[64,512]{1,0:T(8,128)}) %reduce-scatter.5.cloned.1.call-update) | async-done | bytes 131088 | tf_op jit(solution)/shard_map/reduce_scatter | solution.py:40
  407.9 1.1 broadcast_in_dim.61
  409.0 8.5 %all-to-all-start.1 = ((f32[16,32,512]{2,1,0:T(8,128)}), f32[16,32,512]{2,1,0:T(8,128)}, u32[]{:S(2)}, u32[]{:S(2)}) async-start(f32[16,32,512]{2,1,0:T(8,128)} %broadcast_in_dim.61), calls=%async_computation.2 | async-start | bytes 2097152 | tf_op jit(solution)/shard_map/all_to_all | solution.py:9
  418.2 84.2 %all-gather.9.cloned.1.call-done = f32[1024,512]{1,0:T(8,128)} async-done(((f32[64,512]{1,0:T(8,128)}), f32[1024,512]{1,0:T(8,128)}) %all-gather.9.cloned.1.call-update) | async-done | bytes 2097168 | tf_op jit(solution)/shard_map/all_gather | solution.py:41
  502.5 3.4 reshape.168
  505.9 130.8 %all-gather.13.cloned.1.call-done = f32[16384,512]{1,0:T(8,128)} async-done(((f32[512,512]{1,0:T(8,128)}), f32[16384,512]{1,0:T(8,128)}) %all-gather.13.cloned.1.call-update) | async-done | bytes 33554448 | tf_op jit(solution)/shard_map/all_gather | solution.py:25
  636.7 12.3 %reduce.7 = f32[512,512]{1,0:T(8,128)S(1)} reduce(f32[32,512,512]{2,1,0:T(8,128)} %bitcast.60, f32[]{:T(128)} %constant.92.clone.1), dimensions={0}, to_apply=%region_2.4 | reduce | flops 8126464 | bytes 34603012 | tf_op jit(solution)/shard_map/reduce_sum | solution.py:25
  649.0 3.2 convolution_multiply_fusion
  652.2 5.0 bitcast_subtract_fusion
  657.2 2.4 fusion.10
  659.6 1.9 copy.34
  661.5 1.8 copy.35
  (35 shorter events, 2.7 us)
Async XLA Ops:
  6.5 75.1 %reduce-scatter.3.cloned.1.call-start = ((), (), s32[]{:S(2)}) async-start(), calls=%async_computation.4 | async-start | bytes 2228224 | tf_op jit(solution)/shard_map/reduce_scatter | solution.py:40
  12.1 167.9 %all-gather.7.cloned.1.call-start = ((), (), s32[]{:S(2)}) async-start(), calls=%async_computation.5 | async-start | bytes 2228224 | tf_op jit(solution)/shard_map/all_gather | solution.py:41
  81.6 232.0 %all-gather.11.cloned.1.call-start = ((), (), s32[]{:S(2)}) async-start(), calls=%async_computation.8 | async-start | bytes 34603008 | tf_op jit(solution)/shard_map/all_gather | solution.py:25
  83.7 1.4 copy-start.2
  85.1 9.8 %copy-start.3 = (s32[2,16]{1,0:T(2,128)S(1)}, s32[2,16]{1,0:T(2,128)}, u32[]{:S(2)}) copy-start(s32[2,16]{1,0:T(2,128)} %param.12) | copy-start | bytes 388
  86.2 239.7 %all-to-all-start = ((f32[16,32,512]{2,1,0:T(8,128)}), f32[16,32,512]{2,1,0:T(8,128)S(1)}, u32[]{:S(2)}, u32[]{:S(2)}) async-start(f32[16,32,512]{2,1,0:T(8,128)} %broadcast_in_dim.55), calls=%async_computation | async-start | bytes 2097152 | tf_op jit(solution)/shard_map/all_to_all | solution.py:9
  94.7 312.5 %reduce-scatter.5.cloned.1.call-start = ((), (), s32[]{:S(2)}) async-start(), calls=%async_computation.6 | async-start | bytes 2228224 | tf_op jit(solution)/shard_map/reduce_scatter | solution.py:40
  325.9 1.9 copy-start
  344.1 158.4 %all-gather.9.cloned.1.call-start = ((), (), s32[]{:S(2)}) async-start(), calls=%async_computation.7 | async-start | bytes 2228224 | tf_op jit(solution)/shard_map/all_gather | solution.py:41
  407.3 229.4 %all-gather.13.cloned.1.call-start = ((), (), s32[]{:S(2)}) async-start(), calls=%async_computation.9 | async-start | bytes 34603008 | tf_op jit(solution)/shard_map/all_gather | solution.py:25
  409.0 240.0 %all-to-all-start.1 = ((f32[16,32,512]{2,1,0:T(8,128)}), f32[16,32,512]{2,1,0:T(8,128)}, u32[]{:S(2)}, u32[]{:S(2)}) async-start(f32[16,32,512]{2,1,0:T(8,128)} %broadcast_in_dim.61), calls=%async_computation.2 | async-start | bytes 2097152 | tf_op jit(solution)/shard_map/all_to_all | solution.py:9
  649.0 3.2 copy-start.1
Sparse Core Ops, SparseCore 0:
  12.2 69.3 reduce-scatter.2
  83.7 96.2 all-gather.6
  183.2 130.3 all-gather.10
  344.2 63.0 reduce-scatter.4
  409.2 93.2 all-gather.8
  505.4 131.2 all-gather.12

commit v2 on v0

--- a/solution.py
+++ b/solution.py
@@ -38,7 +38,9 @@
     )
     padded = filled_up(lines, lax.axis_size(axis))
     own = lax.psum_scatter(padded, axis, scatter_dimension=0, tiled=True)
-    return lax.all_gather(own, axis, axis=0, tiled=True)[: len(lines)].reshape(value.shape)
+    return jnp.concatenate(
+        lax.all_to_all(jnp.stack([own] * lax.axis_size(axis)), axis, 0, 0), axis=0
+    )[: len(lines)].reshape(value.shape)
 
 
 def apply_pivot(column_part, pivot_rows):

time: 404 us -> 582 us (1.44)
  the two profiles are of different devices: /device:TPU:4 before, /device:TPU:1 now
where the time goes in v2:
time: 582 us; the launch traced here: 581 us
  waiting for transfers between devices  342 us (59%)
  blocking collectives  136 us (23%)
  local copies, waits for them, and re-layouts  36.3 us (6%)
  starting transfers between devices  20 us (3%)
  matrix products  18.9 us (3%)
  between operations  16.3 us (3%)
  other arithmetic  11.5 us (2%)
    psum x2, waiting for transfers between devices, spread(): return lax.psum(kept, axis)  284 us
    all_to_all x2, blocking collectives, copy_for_each(): return lax.all_to_all(copies, axis, split_axis=0, concat_axis=0, tiled=True)  136 us
    reduce_scatter x2, waiting for transfers between devices, broadcast_by_parts(): own = lax.psum_scatter(padded, axis, scatter_dimension=0, tiled=True)  57.6 us
    all_to_all x2, starting transfers between devices, broadcast_by_parts(): lax.all_to_all(jnp.stack([own] * lax.axis_size(axis)), axis, 0, 0)  19.5 us
    dot_general x2, matrix products, outer_update(): jnp.einsum('rbc,cjd->rbjd', lower_part, upper_part, precision=lax.Precisi...  12.5 us
  transfers between devices with their start and end apart: 6, of which 4 were waited for; matrix products, arithmetic and copies ran while one was open for 3% of the time, Pallas kernels for 0%

profile of v2, /device:TPU:1, one launch (start us, length us, event | category | flops | bytes accessed | tf_op | source)
XLA Modules:
  0.0 581.2 jit_solution(6314038819548555872)
XLA Ops:
  7.4 0.8 slice_bitcast_fusion.4
  9.6 1.7 squeeze_reshape.3
  11.4 1.5 multiply_select_fusion.1
  12.9 0.9 copy-done.2
  14.0 70.0 %all_to_all.20 = f32[16,32,512]{2,1,0:T(8,128)} all-to-all(f32[16,32,512]{2,1,0:T(8,128)S(1)} %broadcast_in_dim.55), channel_id=1, replica_groups=mesh['prow'=16,'pcol'=32] {'prow'}, dimensions={0} | all-to-all | bytes 2097152 | tf_op jit(solution)/shard_map/all_to_all | solution.py:9
  84.0 29.2 %reduce-scatter.3.cloned.1.call-done = f32[64,512]{1,0:T(8,128)} async-done(((f32[1024,512]{1,0:T(8,128)}), f32[64,512]{1,0:T(8,128)}) %reduce-scatter.3.cloned.1.call-update) | async-done | bytes 131088 | tf_op jit(solution)/shard_map/reduce_scatter | solution.py:40
  113.2 2.5 stack.4
  115.7 9.4 %all-to-all-start.1 = ((f32[16,64,512]{2,1,0:T(8,128)}), f32[16,64,512]{2,1,0:T(8,128)}, u32[]{:S(2)}, u32[]{:S(2)}) async-start(f32[16,64,512]{2,1,0:T(8,128)} %stack.4), calls=%async_computation.2 | async-start | bytes 4194304 | tf_op jit(solution)/shard_map/all_to_all | solution.py:42
  125.2 2.8 reshape.160
  128.0 2.5 broadcast_select_fusion
  130.5 1.1 copy.28
  131.9 1.8 copy.7
  135.1 3.0 copy.9
  138.3 138.1 %all-reduce.3.cloned.1.call-done = f32[512,512]{1,0:T(8,128)} async-done(((f32[512,512]{1,0:T(8,128)}), f32[512,512]{1,0:T(8,128)}) %all-reduce.3.cloned.1.call-update) | async-done | bytes 1048592 | tf_op jit(solution)/shard_map/psum | solution.py:25
  276.4 3.1 convolution_multiply_fusion.1
  279.5 3.4 reshape_reshape.6
  282.9 5.9 %subtract_bitcast_fusion = f32[1,512,2,512]{3,1,2,0:T(8,128)S(1)} fusion(f32[512,2,512]{2,0,1:T(8,128)} %copy.9, f32[512,2,512]{2,1,0:T(2,128)} %reshape_reshape.6, f32[512,512]{1,0:T(8,128)S(1)} %convolution_multiply_fusion.1), kind=kOutput, calls=%fused_computation.8 | convolution fusion | flops 3221749760 | bytes 7340032 | tf_op jit(solution)/shard_map/rbc,cjd->rbjd/dot_general | solution.py:84
  288.8 1.2 broadcast_select_fusion.1
  290.1 2.9 copy.11
  293.0 3.7 squeeze.35
  296.7 3.1 multiply_select_fusion
  300.0 66.4 %all_to_all.21 = f32[16,32,512]{2,1,0:T(8,128)} all-to-all(f32[16,32,512]{2,1,0:T(8,128)S(1)} %broadcast_in_dim.61), channel_id=1, replica_groups=mesh['prow'=16,'pcol'=32] {'prow'}, dimensions={0} | all-to-all | bytes 2097152 | tf_op jit(solution)/shard_map/all_to_all | solution.py:9
  366.4 28.4 %reduce-scatter.5.cloned.1.call-done = f32[64,512]{1,0:T(8,128)} async-done(((f32[1024,512]{1,0:T(8,128)}), f32[64,512]{1,0:T(8,128)}) %reduce-scatter.5.cloned.1.call-update) | async-done | bytes 131088 | tf_op jit(solution)/shard_map/reduce_scatter | solution.py:40
  394.8 2.5 stack.5
  397.3 10.0 %all-to-all-start.3 = ((f32[16,64,512]{2,1,0:T(8,128)}), f32[16,64,512]{2,1,0:T(8,128)}, u32[]{:S(2)}, u32[]{:S(2)}) async-start(f32[16,64,512]{2,1,0:T(8,128)} %stack.5), calls=%async_computation.5 | async-start | bytes 4194304 | tf_op jit(solution)/shard_map/all_to_all | solution.py:42
  408.5 145.6 %all-reduce.5.cloned.1.call-done = f32[512,512]{1,0:T(8,128)} async-done(((f32[512,512]{1,0:T(8,128)}), f32[512,512]{1,0:T(8,128)}) %all-reduce.5.cloned.1.call-update) | async-done | bytes 1048592 | tf_op jit(solution)/shard_map/psum | solution.py:25
  554.2 3.4 convolution_multiply_fusion
  557.6 3.4 reshape_reshape.7
  561.0 6.6 %bitcast_subtract_fusion = f32[1,512,2,512]{3,1,2,0:T(8,128)} fusion(f32[1,512,2,512]{3,1,2,0:T(8,128)S(1)} %bitcast_dynamic-update-slice_fusion, f32[512,2,512]{2,1,0:T(2,128)} %reshape_reshape.7, f32[512,512]{1,0:T(8,128)S(1)} %convolution_multiply_fusion), kind=kOutput, calls=%fused_computation.2 | convolution fusion | flops 3221749760 | bytes 7340032 | tf_op jit(solution)/shard_map/rbc,cjd->rbjd/dot_general | solution.py:84
  567.6 2.4 fusion.10
  570.0 1.9 copy.14
  571.9 1.8 copy.15
  (32 shorter events, 3.6 us)
Async XLA Ops:
  7.4 105.8 %reduce-scatter.3.cloned.1.call-start = ((), (), s32[]{:S(2)}) async-start(), calls=%async_computation.7 | async-start | bytes 2228224 | tf_op jit(solution)/shard_map/reduce_scatter | solution.py:40
  12.9 0.9 copy-start.2
  115.7 9.5 %copy-start = (f32[512,1024]{1,0:T(8,128)S(1)}, f32[512,1024]{1,0:T(8,128)}, u32[]{:S(2)}) copy-start(f32[512,1024]{1,0:T(8,128)} %param.10) | copy-start | bytes 6291460
  115.7 163.8 %all-to-all-start.1 = ((f32[16,64,512]{2,1,0:T(8,128)}), f32[16,64,512]{2,1,0:T(8,128)}, u32[]{:S(2)}, u32[]{:S(2)}) async-start(f32[16,64,512]{2,1,0:T(8,128)} %stack.4), calls=%async_computation.2 | async-start | bytes 4194304 | tf_op jit(solution)/shard_map/all_to_all | solution.py:42
  125.1 151.3 %all-reduce.3.cloned.1.call-start = ((), (), s32[]{:S(2)}) async-start(), calls=%async_computation.6 | async-start | bytes 2097152 | tf_op jit(solution)/shard_map/psum | solution.py:25
  131.6 263.1 %reduce-scatter.5.cloned.1.call-start = ((), (), s32[]{:S(2)}) async-start(), calls=%async_computation.9 | async-start | bytes 2228224 | tf_op jit(solution)/shard_map/reduce_scatter | solution.py:40
  131.9 1.8 copy-start.3
  135.1 141.3 %copy-start.1 = (f32[16,32,512]{2,1,0:T(8,128)S(1)}, f32[16,32,512]{2,1,0:T(8,128)}, u32[]{:S(2)}) copy-start(f32[16,32,512]{2,1,0:T(8,128)} %all_to_all.20) | copy-start | bytes 3145732
  397.3 160.3 %all-to-all-start.3 = ((f32[16,64,512]{2,1,0:T(8,128)}), f32[16,64,512]{2,1,0:T(8,128)}, u32[]{:S(2)}, u32[]{:S(2)}) async-start(f32[16,64,512]{2,1,0:T(8,128)} %stack.5), calls=%async_computation.5 | async-start | bytes 4194304 | tf_op jit(solution)/shard_map/all_to_all | solution.py:42
  407.3 146.9 %all-reduce.5.cloned.1.call-start = ((), (), s32[]{:S(2)}) async-start(), calls=%async_computation.8 | async-start | bytes 2097152 | tf_op jit(solution)/shard_map/psum | solution.py:25
Sparse Core Ops, SparseCore 0:
  13.1 100.1 reduce-scatter.2
  300.0 94.7 reduce-scatter.4
Sparse Core Ops, SparseCore 1:
  131.7 144.6 all-reduce.2
  411.0 143.1 all-reduce.4
